TPU v7x, 32 devices: a whole 2x2x4 slice. The times are simulated.
32 devices in a mesh: ep: 4 (over y, x), tp: 4 (over z), dp: 2 (over core).
Axes of the slice: x: 2, y: 2, z: 4, core: 2. Of those that a mesh axis runs over, the one named last changes fastest.
Arguments:
- down_weight: bfloat16 [4, 16384, 3072], P('ep', 'tp', 'dp'), may hold values from -130 to 130
- owned_span: int32 [4, 4, 2], replicated, may hold values from 0 to 31, as said below
Outputs:
- saved_spans: bfloat16 [4, 4, 768, 16384], P('ep', 'tp', 'dp')
Inputs may be any that keep to these rules, and one draw needn't show every extreme that they name: `owned_span`: block g holds rows (g % 8) * 384 onward of expert g // 8; every block is stored by exactly one device; the block at [i, j, k] has (g % 8) // 4 == k; for each k the experts of the stored blocks form a Latin square over i and j: each expert once for each i and once for each j.
All inputs are finite; a program needn't handle non-finite values.
Results may differ from a plain program's by a relative error of at most 0.001.
Values may be sent and summed in bfloat16 or wider, within the bound.
A program may use at most 128 MiB of HBM per device.

v0:
```python
import functools

import jax
import jax.numpy as jnp
from jax import lax
from jax.experimental import pallas as pl
from jax.experimental.pallas import tpu as pltpu
from jax.sharding import PartitionSpec as P

MESH = pl.DeviceIdType.MESH
LANES = 128
SUBLANES = 16
CHUNK = 256
STAGES = 4
AHEAD = 2
SPARE = 3 << 20
WRITES = 8


def pick(values, index):
    chosen = values[0]
    for b in range(1, len(values)):
        chosen = jnp.where(index == b, values[b], chosen)
    return chosen


def kernel(n_ep, n_tp, n_dp, chunk, weight, span_hbm, out, stage, turned, send, relay, span,
           load_sem, span_sem, ep_send, ep_recv, tp_send, tp_recv, own_sem, early, middle, spread, late,
           early_send, early_recv, fan_send, fan_recv, late_sem, *arrived):
    my_ep = lax.axis_index("ep")
    my_tp = lax.axis_index("tp")
    my_dp = lax.axis_index("dp")
    hidden, width = weight.shape[1], weight.shape[2]
    rows = width // n_tp
    chunks = hidden // chunk
    per_expert = n_tp * n_dp

    def load(c):
        return pltpu.make_async_copy(
            weight.at[0, pl.ds(c * chunk, chunk)], stage.at[c % STAGES], load_sem.at[c % STAGES])

    def to_ep(c, d):
        return pltpu.make_async_remote_copy(
            send.at[c, d], arrived[c - 1].at[d], ep_send.at[c, d], ep_recv.at[c, d],
            device_id={"ep": lax.rem(my_ep + d, n_ep)}, device_id_type=MESH)

    def columns(tp, c):
        return out.at[0, 0, :, pl.ds(pl.multiple_of(tp * hidden + c * chunk, chunk), chunk)]

    def to_tp(c, d):
        return pltpu.make_async_remote_copy(
            relay.at[c, d], columns(my_tp, c), tp_send.at[c, d], tp_recv.at[c, d],
            device_id={"tp": lax.rem(my_tp + d, n_tp)}, device_id_type=MESH)

    def from_tp(c, d):
        return pltpu.make_async_remote_copy(
            relay.at[c, d], columns(lax.rem(my_tp + n_tp - d, n_tp), c), tp_send.at[c, d], tp_recv.at[c, d],
            device_id={"tp": lax.rem(my_tp + d, n_tp)}, device_id_type=MESH)

    def own(c):
        return pltpu.make_async_copy(relay.at[c, 0], columns(my_tp, c), own_sem.at[c])

    def early_to_tp(d):
        return pltpu.make_async_remote_copy(
            early.at[d - 1], middle.at[d], early_send.at[d], early_recv.at[d],
            device_id={"tp": lax.rem(my_tp + d, n_tp)}, device_id_type=MESH)

    def fan(d):
        return pltpu.make_async_remote_copy(
            middle, spread.at[d - 1], fan_send.at[d], fan_recv.at[d],
            device_id={"ep": lax.rem(my_ep + d, n_ep)}, device_id_type=MESH)

    def late_own(p):
        return pltpu.make_async_copy(late.at[p], columns(lax.rem(my_tp + n_tp - p, n_tp), 0), late_sem.at[p])

    load(0).start()
    span_copy = pltpu.make_async_copy(span_hbm, span, span_sem)
    span_copy.start()

    barrier = pltpu.get_barrier_semaphore()
    for d in range(1, n_ep):
        pl.semaphore_signal(barrier, inc=1, device_id={"ep": lax.rem(my_ep + d, n_ep)}, device_id_type=MESH)
    for d in range(1, n_tp):
        pl.semaphore_signal(barrier, inc=1, device_id={"tp": lax.rem(my_tp + d, n_tp)}, device_id_type=MESH)

    near = my_tp < n_tp // 2
    edge = jnp.where(near, my_tp, n_tp - 1 - my_tp)
    ways = []
    for k in range(n_tp - 1):
        m = k - (n_tp - 1 - 2 * edge)
        half = edge - jnp.maximum(m, 0) // 2
        inner = jnp.where(jnp.maximum(m, 0) % 2 == 0, half, n_tp - half)
        hop = jnp.where(m < 0, n_tp - 1 - edge - k, inner)
        ways.append(jnp.where(near, hop, n_tp - hop))

    span_copy.wait()
    wanted = []
    for d in range(n_ep):
        i = lax.rem(my_ep + d, n_ep)
        total = jnp.int32(0)
        for j in range(n_tp):
            g = span[i, my_dp, j]
            total = total + jnp.where(g // per_expert == my_ep, g % per_expert - my_dp * n_tp, 0)
        wanted.append(total)
    slot = []
    for d in [0] + ways:
        j = lax.rem(my_tp + d, n_tp)
        slot.append(lax.rem(my_ep + n_ep - span[my_ep, my_dp, j] // per_expert, n_ep))

    sooner = []
    for d in [0] + ways:
        j = lax.rem(my_tp + d, n_tp)
        total = jnp.int32(0)
        for i in range(n_ep):
            g = span[i, my_dp, j]
            total = total + jnp.where(g // per_expert == my_ep, g % per_expert - my_dp * n_tp, 0)
        sooner.append(total)

    def turn(c):
        load(c).wait()
        if c == 0:
            for later in range(1, min(STAGES, chunks)):
                load(later).start()

        @pl.loop(0, width // LANES)
        def _(b):
            at = pl.multiple_of(b * LANES, LANES)
            turned[pl.ds(at, LANES), :] = stage[c % STAGES, :, pl.ds(at, LANES)].T

        if c + STAGES < chunks:
            load(c + STAGES).start()

    def block_of(index):
        return pick([turned[b * rows:(b + 1) * rows, :] for b in range(n_tp)], index)

    def first_half(c):
        turn(c)
        for d in range(n_ep - 1, -1, -1):
            if d == 0:
                arrived[c - 1][0] = block_of(wanted[d])
            else:
                send[c, d] = block_of(wanted[d])
                to_ep(c, d).start()

    def second_half(c):
        for d in range(1, n_ep):
            to_ep(c, d).wait_recv()
        for d, index in zip(ways, slot[1:]):
            relay[c, d] = pick([arrived[c - 1][s] for s in range(n_ep)], index)
            to_tp(c, d).start()
        relay[c, 0] = pick([arrived[c - 1][s] for s in range(n_ep)], slot[0])
        own(c).start()

    turn(0)
    for k, d in enumerate(ways):
        early[d - 1] = block_of(sooner[k + 1])
        if k == 0:
            pl.semaphore_wait(barrier, n_ep + n_tp - 2)
        early_to_tp(d).start()
    middle[0] = block_of(sooner[0])

    for step in range(1, chunks + AHEAD):
        if step < chunks:
            first_half(step)
        if step == chunks:
            for d in range(1, n_tp):
                early_to_tp(d).wait_recv()
            for d in range(1, n_ep):
                fan(d).start()
        if step > AHEAD:
            second_half(step - AHEAD)

    for d in range(1, n_ep):
        fan(d).wait_recv()
    for p in range(n_tp):
        late[p] = pick([middle[p]] + [spread[d - 1, p] for d in range(1, n_ep)], slot[0])
        late_own(p).start()

    for d in range(1, n_ep):
        fan(d).wait_send()
    for d in range(1, n_tp):
        early_to_tp(d).wait_send()
    for c in range(1, chunks):
        for d in range(1, n_ep):
            to_ep(c, d).wait_send()
        for d in range(1, n_tp):
            from_tp(c, d).wait_recv()
            to_tp(c, d).wait_send()
        own(c).wait()
    for p in range(n_tp):
        late_own(p).wait()


def writer(saved, out, sem):
    pieces = sem.shape[0]
    rows = saved.shape[2] // pieces
    copies = [
        pltpu.make_async_copy(
            saved.at[0, 0, pl.ds(p * rows, rows)], out.at[0, 0, pl.ds(p * rows, rows)], sem.at[p])
        for p in range(pieces)
    ]
    for copy in copies:
        copy.start()
    for copy in copies:
        copy.wait()


def write_out(saved):
    tiles = max(saved.shape[2] // SUBLANES, 1)
    pieces = max(p for p in range(1, WRITES + 1) if tiles % p == 0)
    return pl.pallas_call(
        writer,
        out_shape=jax.ShapeDtypeStruct(saved.shape, saved.dtype),
        in_specs=[pl.BlockSpec(memory_space=pltpu.VMEM)],
        out_specs=pl.BlockSpec(memory_space=pl.ANY),
        scratch_shapes=[pltpu.SemaphoreType.DMA((pieces,))],
        compiler_params=pltpu.CompilerParams(vmem_limit_bytes=SPARE),
    )(saved)


def local(down_weight, owned_span):
    n_ep, n_tp, n_dp = (lax.axis_size(a) for a in ("ep", "tp", "dp"))
    _, hidden, width = down_weight.shape
    rows = width // n_tp
    chunk = min(CHUNK, hidden)
    chunks = hidden // chunk
    kind = down_weight.dtype
    block = rows * chunk * kind.itemsize
    scratch_bytes = (STAGES + 1) * n_tp * block + chunks * (2 * n_ep + n_tp) * block + (n_ep + 2) * n_tp * block
    saved = pl.pallas_call(
        functools.partial(kernel, n_ep, n_tp, n_dp, chunk),
        out_shape=pltpu.VMEM((1, 1, rows, n_tp * hidden), kind),
        in_specs=[pl.BlockSpec(memory_space=pl.ANY), pl.BlockSpec(memory_space=pl.ANY)],
        out_specs=pl.BlockSpec(memory_space=pltpu.VMEM),
        scratch_shapes=[
            pltpu.VMEM((STAGES, chunk, width), kind),
            pltpu.VMEM((width, chunk), kind),
            pltpu.VMEM((chunks, n_ep, rows, chunk), kind),
            pltpu.VMEM((chunks, n_tp, rows, chunk), kind),
            pltpu.SMEM((n_ep, n_dp, n_tp), jnp.int32),
            pltpu.SemaphoreType.DMA((STAGES,)),
            pltpu.SemaphoreType.DMA,
            pltpu.SemaphoreType.DMA((chunks, n_ep)),
            pltpu.SemaphoreType.DMA((chunks, n_ep)),
            pltpu.SemaphoreType.DMA((chunks, n_tp)),
            pltpu.SemaphoreType.DMA((chunks, n_tp)),
            pltpu.SemaphoreType.DMA((chunks,)),
            pltpu.VMEM((n_tp - 1, rows, chunk), kind),
            pltpu.VMEM((n_tp, rows, chunk), kind),
            pltpu.VMEM((n_ep - 1, n_tp, rows, chunk), kind),
            pltpu.VMEM((n_tp, rows, chunk), kind),
            pltpu.SemaphoreType.DMA((n_tp,)),
            pltpu.SemaphoreType.DMA((n_tp,)),
            pltpu.SemaphoreType.DMA((n_ep,)),
            pltpu.SemaphoreType.DMA((n_ep,)),
            pltpu.SemaphoreType.DMA((n_tp,)),
        ] + [pltpu.VMEM((n_ep, rows, chunk), kind) for _ in range(chunks - 1)],
        compiler_params=pltpu.CompilerParams(
            collective_id=0, has_side_effects=True, vmem_limit_bytes=scratch_bytes + SPARE),
    )(down_weight, jnp.transpose(owned_span, (0, 2, 1)))
    return write_out(saved)


def solution(mesh):
    return jax.shard_map(
        local,
        mesh=mesh,
        in_specs=(P("ep", "tp", "dp"), P()),
        out_specs=P("ep", "tp", "dp", None),
        check_vma=False,
    )
```

profile of v0, /device:TPU:12, one launch (start us, length us, event | category | flops | bytes accessed | tf_op | source)
XLA Modules:
  0.0 281.5 jit_solution(13417065282242958505)
XLA Ops:
  0.0 276.9 %shard_map.28.saved = bf16[1,1,384,16384]{3,2,1,0:T(8,128)(2,1)S(1)} custom-call(bf16[1,4096,1536]{2,1,0:T(8,128)(2,1)} %weight.1, s32[4,2,4]{2,1,0:T(2,128)} %bitcast.1), custom_call_target="tpu_custom_call" | custom-call | tf_op jit(solution)/shard_map/pallas_call | solution.py:230
  276.9 4.7 %shard_map.29 = bf16[1,1,384,16384]{3,2,1,0:T(8,128)(2,1)} custom-call(bf16[1,1,384,16384]{3,2,1,0:T(8,128)(2,1)S(1)} %shard_map.28.saved), custom_call_target="tpu_custom_call" | custom-call | tf_op jit(solution)/shard_map/pallas_call | solution.py:211
where the time goes:
time: 282 us
  Pallas kernels  282 us (100%)
    pallas_call x1, Pallas kernels, local(): pl.pallas_call(functools.partial(kernel, n_ep, n_tp, n_dp, chunk), out_sh...  277 us

commit v1 on v0

--- a/solution.py
+++ b/solution.py
@@ -15,6 +15,7 @@
 AHEAD = 2
 SPARE = 3 << 20
 WRITES = 8
+KEEP = (1, 5)
 
 
 def pick(values, index):
@@ -24,7 +25,15 @@
     return chosen
 
 
-def kernel(n_ep, n_tp, n_dp, chunk, weight, span_hbm, out, stage, turned, send, relay, span,
+def middle_of(my_tp, n_tp):
+    return jnp.logical_or(my_tp == n_tp // 2 - 1, my_tp == n_tp // 2)
+
+
+def kept_by(my_dp, most):
+    return jnp.where(my_dp % 2 == 0, min(KEEP[0], most), min(KEEP[1], most))
+
+
+def kernel(n_ep, n_tp, n_dp, chunk, most, weight, span_hbm, out, kept, stage, turned, send, relay, span,
            load_sem, span_sem, ep_send, ep_recv, tp_send, tp_recv, own_sem, early, middle, spread, late,
            early_send, early_recv, fan_send, fan_recv, late_sem, *arrived):
     my_ep = lax.axis_index("ep")
@@ -34,6 +43,7 @@
     rows = width // n_tp
     chunks = hidden // chunk
     per_expert = n_tp * n_dp
+    keep = kept_by(my_dp, most)
 
     def load(c):
         return pltpu.make_async_copy(
@@ -145,9 +155,16 @@
     def second_half(c):
         for d in range(1, n_ep):
             to_ep(c, d).wait_recv()
-        for d, index in zip(ways, slot[1:]):
-            relay[c, d] = pick([arrived[c - 1][s] for s in range(n_ep)], index)
-            to_tp(c, d).start()
+        for k, (d, index) in enumerate(zip(ways, slot[1:])):
+            piece = pick([arrived[c - 1][s] for s in range(n_ep)], index)
+            relay[c, d] = piece
+            p = chunks - 1 - c
+            if k == n_tp - 3 and p < most:
+                kept[p] = piece
+                stays = jnp.logical_and(edge == n_tp // 2 - 1, p < keep)
+                pl.when(jnp.logical_not(stays))(to_tp(c, d).start)
+            else:
+                to_tp(c, d).start()
         relay[c, 0] = pick([arrived[c - 1][s] for s in range(n_ep)], slot[0])
         own(c).start()
 
@@ -184,14 +201,21 @@
         for d in range(1, n_ep):
             to_ep(c, d).wait_send()
         for d in range(1, n_tp):
-            from_tp(c, d).wait_recv()
-            to_tp(c, d).wait_send()
+            p = chunks - 1 - c
+            if p < most and d in (1, n_tp - 1):
+                low, high = my_tp == n_tp // 2 - 1, my_tp == n_tp // 2
+                sent, got = (low, high) if d == 1 else (high, low)
+                pl.when(jnp.logical_not(jnp.logical_and(got, p < keep)))(from_tp(c, d).wait_recv)
+                pl.when(jnp.logical_not(jnp.logical_and(sent, p < keep)))(to_tp(c, d).wait_send)
+            else:
+                from_tp(c, d).wait_recv()
+                to_tp(c, d).wait_send()
         own(c).wait()
     for p in range(n_tp):
         late_own(p).wait()
 
 
-def writer(saved, out, sem):
+def writer(saved, out, token, sem):
     pieces = sem.shape[0]
     rows = saved.shape[2] // pieces
     copies = [
@@ -203,6 +227,7 @@
         copy.start()
     for copy in copies:
         copy.wait()
+    token[...] = jnp.zeros_like(token)
 
 
 def write_out(saved):
@@ -210,12 +235,78 @@
     pieces = max(p for p in range(1, WRITES + 1) if tiles % p == 0)
     return pl.pallas_call(
         writer,
-        out_shape=jax.ShapeDtypeStruct(saved.shape, saved.dtype),
+        out_shape=(jax.ShapeDtypeStruct(saved.shape, saved.dtype), pltpu.VMEM((8, LANES), jnp.float32)),
         in_specs=[pl.BlockSpec(memory_space=pltpu.VMEM)],
-        out_specs=pl.BlockSpec(memory_space=pl.ANY),
+        out_specs=(pl.BlockSpec(memory_space=pl.ANY), pl.BlockSpec(memory_space=pltpu.VMEM)),
         scratch_shapes=[pltpu.SemaphoreType.DMA((pieces,))],
         compiler_params=pltpu.CompilerParams(vmem_limit_bytes=SPARE),
     )(saved)
+
+
+def swap(n_tp, kept, token, got, send_sem, recv_sem):
+    my_tp = lax.axis_index("tp")
+    other = n_tp - 1 - my_tp
+    most = kept.shape[0]
+    keep = kept_by(lax.axis_index("dp"), most)
+
+    @pl.when(middle_of(my_tp, n_tp))
+    def _():
+        barrier = pltpu.get_barrier_semaphore()
+        pl.semaphore_signal(barrier, inc=1, device_id={"tp": other}, device_id_type=MESH)
+        pl.semaphore_wait(barrier, 1)
+        copies = [
+            pltpu.make_async_remote_copy(
+                kept.at[p], got.at[p], send_sem.at[p], recv_sem.at[p],
+                device_id={"tp": other}, device_id_type=MESH)
+            for p in range(most)
+        ]
+        for p in reversed(range(most)):
+            pl.when(p < keep)(copies[p].start)
+        for p in reversed(range(most)):
+            pl.when(p < keep)(copies[p].wait)
+
+
+def exchange(n_tp, kept, token):
+    return pl.pallas_call(
+        functools.partial(swap, n_tp),
+        out_shape=pltpu.VMEM(kept.shape, kept.dtype),
+        in_specs=[pl.BlockSpec(memory_space=pltpu.VMEM)] * 2,
+        out_specs=pl.BlockSpec(memory_space=pltpu.VMEM),
+        scratch_shapes=[pltpu.SemaphoreType.DMA((kept.shape[0],)), pltpu.SemaphoreType.DMA((kept.shape[0],))],
+        compiler_params=pltpu.CompilerParams(collective_id=1, has_side_effects=True, vmem_limit_bytes=SPARE),
+    )(kept, token)
+
+
+def finish(n_tp, hidden, got, written, out, sem):
+    del written
+    my_tp = lax.axis_index("tp")
+    most, _, chunk = got.shape
+    keep = kept_by(lax.axis_index("dp"), most)
+
+    @pl.when(middle_of(my_tp, n_tp))
+    def _():
+        end = (n_tp - my_tp) * hidden
+        copies = [
+            pltpu.make_async_copy(
+                got.at[p], out.at[0, 0, :, pl.ds(pl.multiple_of(end - (p + 1) * chunk, chunk), chunk)], sem.at[p])
+            for p in range(most)
+        ]
+        for p in range(most):
+            pl.when(p < keep)(copies[p].start)
+        for p in range(most):
+            pl.when(p < keep)(copies[p].wait)
+
+
+def write_rest(n_tp, hidden, got, written):
+    return pl.pallas_call(
+        functools.partial(finish, n_tp, hidden),
+        out_shape=jax.ShapeDtypeStruct(written.shape, written.dtype),
+        in_specs=[pl.BlockSpec(memory_space=pltpu.VMEM), pl.BlockSpec(memory_space=pl.ANY)],
+        out_specs=pl.BlockSpec(memory_space=pl.ANY),
+        scratch_shapes=[pltpu.SemaphoreType.DMA((got.shape[0],))],
+        input_output_aliases={1: 0},
+        compiler_params=pltpu.CompilerParams(vmem_limit_bytes=SPARE),
+    )(got, written)
 
 
 def local(down_weight, owned_span):
@@ -224,14 +315,15 @@
     rows = width // n_tp
     chunk = min(CHUNK, hidden)
     chunks = hidden // chunk
+    most = min(max(KEEP), chunks - 1)
     kind = down_weight.dtype
     block = rows * chunk * kind.itemsize
     scratch_bytes = (STAGES + 1) * n_tp * block + chunks * (2 * n_ep + n_tp) * block + (n_ep + 2) * n_tp * block
-    saved = pl.pallas_call(
-        functools.partial(kernel, n_ep, n_tp, n_dp, chunk),
-        out_shape=pltpu.VMEM((1, 1, rows, n_tp * hidden), kind),
+    saved, kept = pl.pallas_call(
+        functools.partial(kernel, n_ep, n_tp, n_dp, chunk, most),
+        out_shape=(pltpu.VMEM((1, 1, rows, n_tp * hidden), kind), pltpu.VMEM((most, rows, chunk), kind)),
         in_specs=[pl.BlockSpec(memory_space=pl.ANY), pl.BlockSpec(memory_space=pl.ANY)],
-        out_specs=pl.BlockSpec(memory_space=pltpu.VMEM),
+        out_specs=(pl.BlockSpec(memory_space=pltpu.VMEM), pl.BlockSpec(memory_space=pltpu.VMEM)),
         scratch_shapes=[
             pltpu.VMEM((STAGES, chunk, width), kind),
             pltpu.VMEM((width, chunk), kind),
@@ -258,7 +350,8 @@
         compiler_params=pltpu.CompilerParams(
             collective_id=0, has_side_effects=True, vmem_limit_bytes=scratch_bytes + SPARE),
     )(down_weight, jnp.transpose(owned_span, (0, 2, 1)))
-    return write_out(saved)
+    written, token = write_out(saved)
+    return write_rest(n_tp, hidden, exchange(n_tp, kept, token), written)
 
 
 def solution(mesh):

time: 282 us -> 275 us (0.975)
  Pallas kernels: 282 us -> 275 us
    pallas_call x2 -> x4, Pallas kernels: 282 us -> 275 us  [the longest x1 262 us: local(): pl.pallas_call(functools.partial(kernel, n_ep, n_tp, n_dp, chunk, most),...]
where the time goes in v1:
time: 275 us
  Pallas kernels  275 us (100%)
    pallas_call x1, Pallas kernels, local(): pl.pallas_call(functools.partial(kernel, n_ep, n_tp, n_dp, chunk, most),...  262 us
    pallas_call x1, Pallas kernels, exchange(): pl.pallas_call(functools.partial(swap, n_tp), out_shape=pltpu.VMEM(kept.s...  7.21 us

profile of v1, /device:TPU:12, one launch (start us, length us, event | category | flops | bytes accessed | tf_op | source)
XLA Modules:
  0.0 275.0 jit_solution(11170274130865098633)
XLA Ops:
  0.0 262.4 %shard_map.28 = (bf16[1,1,384,16384]{3,2,1,0:T(8,128)(2,1)S(1)}, bf16[5,384,256]{2,1,0:T(8,128)(2,1)S(1)}) custom-call(bf16[1,4096,1536]{2,1,0:T(8,128)(2,1)} %weight.1, s32[4,2,4]{2,1,0:T(2,128)} %bitcast.1), custom_call_target="tpu_custom_call" | custom-call | tf_op jit(solution)/shard_map/pallas_call | solution.py:322
  262.4 4.7 %shard_map.29 = (bf16[1,1,384,16384]{3,2,1,0:T(8,128)(2,1)}, f32[8,128]{1,0:T(8,128)S(1)}) custom-call(bf16[1,1,384,16384]{3,2,1,0:T(8,128)(2,1)S(1)} %get-tuple-element.10.saved), custom_call_target="tpu_custom_call" | custom-call | tf_op jit(solution)/shard_map/pallas_call | solution.py:236
  267.1 7.2 %shard_map.30.got = bf16[5,384,256]{2,1,0:T(8,128)(2,1)S(1)} custom-call(bf16[5,384,256]{2,1,0:T(8,128)(2,1)S(1)} %get-tuple-element.9.kept, f32[8,128]{1,0:T(8,128)S(1)} %get-tuple-element.11.token), custom_call_target="tpu_custom_call" | custom-call | tf_op jit(solution)/shard_map/pallas_call | solution.py:270
  274.3 0.7 shard_map.31

commit v2 on v1

v2 whole, which is shorter than its diff:
```python
import functools

import jax
import jax.numpy as jnp
from jax import lax
from jax.experimental import pallas as pl
from jax.experimental.pallas import tpu as pltpu
from jax.sharding import PartitionSpec as P

MESH = pl.DeviceIdType.MESH
LANES = 128
SUBLANES = 16
CHUNK = 256
STAGES = 4
AHEAD = 2
SPARE = 3 << 20
VMEM_BYTES = 67043328
WRITES = 8
KEEP = (2, 5)


def pick(values, index):
    chosen = values[0]
    for b in range(1, len(values)):
        chosen = jnp.where(index == b, values[b], chosen)
    return chosen


def middle_of(my_tp, n_tp):
    return jnp.logical_or(my_tp == n_tp // 2 - 1, my_tp == n_tp // 2)


def kept_by(my_dp, most):
    return jnp.where(my_dp % 2 == 0, min(KEEP[0], most), min(KEEP[1], most))


def kept_counts(most):
    return sorted({min(k, most) for k in KEEP})


def kernel(n_ep, n_tp, n_dp, chunk, most, weight, span_hbm, out, kept, stage, turned, send, relay, span,
           early, middle, spread, load_sem, span_sem, ep_send, ep_recv, tp_send, tp_recv, late_send, late_recv,
           early_send, early_recv, fan_send, fan_recv, *arrived):
    my_ep = lax.axis_index("ep")
    my_tp = lax.axis_index("tp")
    my_dp = lax.axis_index("dp")
    hidden, width = weight.shape[1], weight.shape[2]
    rows = width // n_tp
    chunks = hidden // chunk
    per_expert = n_tp * n_dp
    keep = kept_by(my_dp, most)
    mid = middle_of(my_tp, n_tp)
    others = jnp.logical_not(mid)

    near = my_tp < n_tp // 2
    edge = jnp.where(near, my_tp, n_tp - 1 - my_tp)
    ways = []
    for k in range(n_tp - 1):
        m = k - (n_tp - 1 - 2 * edge)
        half = edge - jnp.maximum(m, 0) // 2
        inner = jnp.where(jnp.maximum(m, 0) % 2 == 0, half, n_tp - half)
        hop = jnp.where(m < 0, n_tp - 1 - edge - k, inner)
        ways.append(jnp.where(near, hop, n_tp - hop))
    across = n_tp - 3

    def load(c):
        return pltpu.make_async_copy(
            weight.at[0, pl.ds(c * chunk, chunk)], stage.at[c % STAGES], load_sem.at[c % STAGES])

    def remote(src, dst, send_sem, recv_sem, axis, d, n):
        me = my_ep if axis == "ep" else my_tp
        return pltpu.make_async_remote_copy(
            src, dst, send_sem, recv_sem, device_id={axis: lax.rem(me + d, n)}, device_id_type=MESH)

    def to_ep(c, d):
        return remote(send.at[(c - 1) * (n_ep - 1) + d - 1], arrived[c - 1].at[d], ep_send, ep_recv.at[c - 1], "ep", d, n_ep)

    def columns(tp, c):
        return pl.ds(pl.multiple_of(tp * hidden + c * chunk, chunk), chunk)

    def to_tp(c, k, send_sem, recv_sem):
        return remote(
            relay.at[(c - 1) * (n_tp - 1) + k], out.at[0, 0, :, columns(my_tp, c)], send_sem, recv_sem, "tp", ways[k], n_tp)

    def early_to_tp(k):
        return remote(early.at[k], middle.at[ways[k]], early_send, early_recv, "tp", ways[k], n_tp)

    def fan(d):
        return remote(middle, spread.at[d - 1], fan_send, fan_recv, "ep", d, n_ep)

    def ep_sent():
        return remote(send, send, ep_send, ep_recv.at[0], "ep", 1, n_ep)

    def ep_got(c):
        here = arrived[c - 1].at[pl.ds(1, n_ep - 1)]
        return remote(here, here, ep_send, ep_recv.at[c - 1], "ep", 1, n_ep)

    def all_tp(blocks):
        return remote(
            relay.at[pl.ds(0, blocks)], out.at[0, 0, :, pl.ds(0, blocks * chunk)], tp_send, tp_recv, "tp", 1, n_tp)

    def all_early():
        return remote(early, middle.at[pl.ds(1, n_tp - 1)], early_send, early_recv, "tp", 1, n_tp)

    def all_fan():
        return remote(spread, spread, fan_send, fan_recv, "ep", 1, n_ep)

    load(0).start()
    barrier = pltpu.get_barrier_semaphore()
    for d in range(1, n_tp):
        pl.semaphore_signal(barrier, inc=1, device_id={"tp": lax.rem(my_tp + d, n_tp)}, device_id_type=MESH)
    for d in range(n_ep - 1, 0, -1):
        pl.semaphore_signal(barrier, inc=1, device_id={"ep": lax.rem(my_ep + d, n_ep)}, device_id_type=MESH)
    span_copy = pltpu.make_async_copy(span_hbm, span, span_sem)
    span_copy.start()
    span_copy.wait()

    wanted = []
    for d in range(n_ep):
        i = lax.rem(my_ep + d, n_ep)
        total = jnp.int32(0)
        for j in range(n_tp):
            g = span[i, my_dp, j]
            total = total + jnp.where(g // per_expert == my_ep, g % per_expert - my_dp * n_tp, 0)
        wanted.append(total)
    slot = []
    for d in [0] + ways:
        j = lax.rem(my_tp + d, n_tp)
        slot.append(lax.rem(my_ep + n_ep - span[my_ep, my_dp, j] // per_expert, n_ep))

    sooner = []
    for d in [0] + ways:
        j = lax.rem(my_tp + d, n_tp)
        total = jnp.int32(0)
        for i in range(n_ep):
            g = span[i, my_dp, j]
            total = total + jnp.where(g // per_expert == my_ep, g % per_expert - my_dp * n_tp, 0)
        sooner.append(total)

    def turn(c):
        load(c).wait()

        @pl.loop(0, width // LANES)
        def _(b):
            at = pl.multiple_of(b * LANES, LANES)
            turned[pl.ds(at, LANES), :] = stage[c % STAGES, :, pl.ds(at, LANES)].T

        if c + STAGES < chunks:
            load(c + STAGES).start()

    def block_of(index):
        return pick([turned[b * rows:(b + 1) * rows, :] for b in range(n_tp)], index)

    def first_block(target, index):
        if rows % LANES:
            target[...] = block_of(index)
            return
        for q in range(0, rows, LANES):
            tiles = [stage[0, :, b * rows + q:b * rows + q + LANES] for b in range(n_tp)]
            target[q:q + LANES, :] = pick(tiles, index).T

    def first_half(c):
        turn(c)
        for d in range(n_ep - 1, -1, -1):
            if d == 0:
                arrived[c - 1][0] = block_of(wanted[d])
            else:
                send[(c - 1) * (n_ep - 1) + d - 1] = block_of(wanted[d])
                to_ep(c, d).start()

    def second_half(c):
        ep_got(c).wait_recv()
        p = chunks - 1 - c
        for k in range(n_tp - 1):
            piece = pick([arrived[c - 1][s] for s in range(n_ep)], slot[k + 1])
            relay[(c - 1) * (n_tp - 1) + k] = piece
            if k == across and p < most:
                kept[:, (most - 1 - p) * chunk:(most - p) * chunk] = piece
                pl.when(others)(to_tp(c, k, tp_send, tp_recv).start)
                pl.when(jnp.logical_and(mid, p >= keep))(to_tp(c, k, late_send.at[p], late_recv.at[p]).start)
            else:
                to_tp(c, k, tp_send, tp_recv).start()
        out[0, 0, :, columns(my_tp, c)] = pick([arrived[c - 1][s] for s in range(n_ep)], slot[0])

    if rows % LANES:
        turn(0)
    else:
        load(0).wait()
    for later in range(1, min(STAGES, chunks)):
        load(later).start()
    for k in range(n_tp - 1):
        first_block(early.at[k], sooner[k + 1])
        if k == 0:
            pl.semaphore_wait(barrier, n_ep + n_tp - 2)
        early_to_tp(k).start()
    first_block(middle.at[0], sooner[0])
    if rows % LANES == 0 and STAGES < chunks:
        load(STAGES).start()

    for step in range(1, chunks + AHEAD):
        if step < chunks:
            first_half(step)
        if step == chunks:
            all_early().wait_recv()
            for d in range(1, n_ep):
                fan(d).start()
        if step > AHEAD:
            second_half(step - AHEAD)

    all_fan().wait_recv()
    for p in range(n_tp):
        found = pick([middle[p]] + [spread[d - 1, p] for d in range(1, n_ep)], slot[0])
        out[0, 0, :, columns(lax.rem(my_tp + n_tp - p, n_tp), 0)] = found

    all_fan().wait_send()
    all_early().wait_send()
    ep_sent().wait_send()
    blocks = (chunks - 1) * (n_tp - 1)

    @pl.when(others)
    def _():
        all_tp(blocks).wait()

    @pl.when(mid)
    def _():
        all_tp(blocks - most).wait()

    for p in range(most):
        pl.when(jnp.logical_and(mid, p >= keep))(
            to_tp(chunks - 1 - p, across, late_send.at[p], late_recv.at[p]).wait)


def writer(saved, out, token, sem):
    pieces = sem.shape[0]
    rows = saved.shape[2] // pieces
    copies = [
        pltpu.make_async_copy(
            saved.at[0, 0, pl.ds(p * rows, rows)], out.at[0, 0, pl.ds(p * rows, rows)], sem.at[p])
        for p in range(pieces)
    ]
    for copy in copies:
        copy.start()
    for copy in copies:
        copy.wait()
    token[...] = jnp.zeros_like(token)


def write_out(saved):
    tiles = max(saved.shape[2] // SUBLANES, 1)
    pieces = max(p for p in range(1, WRITES + 1) if tiles % p == 0)
    return pl.pallas_call(
        writer,
        out_shape=(jax.ShapeDtypeStruct(saved.shape, saved.dtype), pltpu.VMEM((8, LANES), jnp.float32)),
        in_specs=[pl.BlockSpec(memory_space=pltpu.VMEM)],
        out_specs=(pl.BlockSpec(memory_space=pl.ANY), pl.BlockSpec(memory_space=pltpu.VMEM)),
        scratch_shapes=[pltpu.SemaphoreType.DMA((pieces,))],
        compiler_params=pltpu.CompilerParams(vmem_limit_bytes=SPARE),
    )(saved)


def swap(n_tp, chunk, kept, token, got, send_sem, recv_sem):
    del token
    my_tp = lax.axis_index("tp")
    other = n_tp - 1 - my_tp
    most = kept.shape[1] // chunk
    keep = kept_by(lax.axis_index("dp"), most)

    @pl.when(middle_of(my_tp, n_tp))
    def _():
        barrier = pltpu.get_barrier_semaphore()
        pl.semaphore_signal(barrier, inc=1, device_id={"tp": other}, device_id_type=MESH)
        pl.semaphore_wait(barrier, 1)
        for count in kept_counts(most):
            part = pl.ds((most - count) * chunk, count * chunk)
            copy = pltpu.make_async_remote_copy(
                kept.at[:, part], got.at[:, part], send_sem, recv_sem,
                device_id={"tp": other}, device_id_type=MESH)
            pl.when(keep == count)(copy.start)
        for count in kept_counts(most):
            part = pl.ds((most - count) * chunk, count * chunk)
            copy = pltpu.make_async_remote_copy(
                kept.at[:, part], got.at[:, part], send_sem, recv_sem,
                device_id={"tp": other}, device_id_type=MESH)
            pl.when(keep == count)(copy.wait)


def exchange(n_tp, chunk, kept, token):
    return pl.pallas_call(
        functools.partial(swap, n_tp, chunk),
        out_shape=pltpu.VMEM(kept.shape, kept.dtype),
        in_specs=[pl.BlockSpec(memory_space=pltpu.VMEM)] * 2,
        out_specs=pl.BlockSpec(memory_space=pltpu.VMEM),
        scratch_shapes=[pltpu.SemaphoreType.DMA, pltpu.SemaphoreType.DMA],
        compiler_params=pltpu.CompilerParams(collective_id=1, has_side_effects=True, vmem_limit_bytes=SPARE),
    )(kept, token)


def finish(n_tp, hidden, chunk, got, written, out, sem):
    del written
    my_tp = lax.axis_index("tp")
    most = got.shape[1] // chunk
    keep = kept_by(lax.axis_index("dp"), most)
    end = (n_tp - my_tp) * hidden

    @pl.when(middle_of(my_tp, n_tp))
    def _():
        for count in kept_counts(most):
            size = count * chunk
            copy = pltpu.make_async_copy(
                got.at[:, pl.ds((most - count) * chunk, size)],
                out.at[0, 0, :, pl.ds(pl.multiple_of(end - size, chunk), size)], sem)

            @pl.when(keep == count)
            def _():
                copy.start()
                copy.wait()


def write_rest(n_tp, hidden, chunk, got, written):
    return pl.pallas_call(
        functools.partial(finish, n_tp, hidden, chunk),
        out_shape=jax.ShapeDtypeStruct(written.shape, written.dtype),
        in_specs=[pl.BlockSpec(memory_space=pltpu.VMEM), pl.BlockSpec(memory_space=pl.ANY)],
        out_specs=pl.BlockSpec(memory_space=pl.ANY),
        scratch_shapes=[pltpu.SemaphoreType.DMA],
        input_output_aliases={1: 0},
        compiler_params=pltpu.CompilerParams(vmem_limit_bytes=SPARE),
    )(got, written)


def local(down_weight, owned_span):
    n_ep, n_tp, n_dp = (lax.axis_size(a) for a in ("ep", "tp", "dp"))
    _, hidden, width = down_weight.shape
    rows = width // n_tp
    chunk = min(CHUNK, hidden)
    chunks = hidden // chunk
    most = min(max(KEEP), chunks - 1)
    kind = down_weight.dtype
    results = (n_tp * hidden + most * chunk) * rows * kind.itemsize
    saved, kept = pl.pallas_call(
        functools.partial(kernel, n_ep, n_tp, n_dp, chunk, most),
        out_shape=(pltpu.VMEM((1, 1, rows, n_tp * hidden), kind), pltpu.VMEM((rows, most * chunk), kind)),
        in_specs=[pl.BlockSpec(memory_space=pl.ANY), pl.BlockSpec(memory_space=pl.ANY)],
        out_specs=(pl.BlockSpec(memory_space=pltpu.VMEM), pl.BlockSpec(memory_space=pltpu.VMEM)),
        scratch_shapes=[
            pltpu.VMEM((STAGES, chunk, width), kind),
            pltpu.VMEM((width, chunk), kind),
            pltpu.VMEM(((chunks - 1) * (n_ep - 1), rows, chunk), kind),
            pltpu.VMEM(((chunks - 1) * (n_tp - 1), rows, chunk), kind),
            pltpu.SMEM((n_ep, n_dp, n_tp), jnp.int32),
            pltpu.VMEM((n_tp - 1, rows, chunk), kind),
            pltpu.VMEM((n_tp, rows, chunk), kind),
            pltpu.VMEM((n_ep - 1, n_tp, rows, chunk), kind),
            pltpu.SemaphoreType.DMA((STAGES,)),
            pltpu.SemaphoreType.DMA,
            pltpu.SemaphoreType.DMA,
            pltpu.SemaphoreType.DMA((chunks - 1,)),
            pltpu.SemaphoreType.DMA,
            pltpu.SemaphoreType.DMA,
            pltpu.SemaphoreType.DMA((most,)),
            pltpu.SemaphoreType.DMA((most,)),
            pltpu.SemaphoreType.DMA,
            pltpu.SemaphoreType.DMA,
            pltpu.SemaphoreType.DMA,
            pltpu.SemaphoreType.DMA,
        ] + [pltpu.VMEM((n_ep, rows, chunk), kind) for _ in range(chunks - 1)],
        compiler_params=pltpu.CompilerParams(
            collective_id=0, has_side_effects=True, vmem_limit_bytes=VMEM_BYTES - results),
    )(down_weight, jnp.transpose(owned_span, (0, 2, 1)))
    written, token = write_out(saved)
    return write_rest(n_tp, hidden, chunk, exchange(n_tp, chunk, kept, token), written)


def solution(mesh):
    return jax.shard_map(
        local,
        mesh=mesh,
        in_specs=(P("ep", "tp", "dp"), P()),
        out_specs=P("ep", "tp", "dp", None),
        check_vma=False,
    )
```

time: 275 us -> 275 us (level)
    pallas_call x1, Pallas kernels: 262 us -> 259 us  [local(): pl.pallas_call(functools.partial(kernel, n_ep, n_tp, n_dp, chunk, most),...]
where the time goes in v2:
time: 275 us; the launch traced here: 274 us
  Pallas kernels  274 us (100%)
    pallas_call x1, Pallas kernels, local(): pl.pallas_call(functools.partial(kernel, n_ep, n_tp, n_dp, chunk, most),...  259 us
    pallas_call x1, Pallas kernels, exchange(): pl.pallas_call(functools.partial(swap, n_tp, chunk), out_shape=pltpu.VMEM...  9.2 us

profile of v2, /device:TPU:12, one launch (start us, length us, event | category | flops | bytes accessed | tf_op | source)
XLA Modules:
  0.0 274.0 jit_solution(10598098463092012386)
XLA Ops:
  0.0 259.4 %shard_map.28 = (bf16[1,1,384,16384]{3,2,1,0:T(8,128)(2,1)S(1)}, bf16[384,1280]{1,0:T(8,128)(2,1)S(1)}) custom-call(bf16[1,4096,1536]{2,1,0:T(8,128)(2,1)} %weight.1, s32[4,2,4]{2,1,0:T(2,128)} %bitcast.1), custom_call_target="tpu_custom_call" | custom-call | tf_op jit(solution)/shard_map/pallas_call | solution.py:340
  259.4 4.7 %shard_map.29 = (bf16[1,1,384,16384]{3,2,1,0:T(8,128)(2,1)}, f32[8,128]{1,0:T(8,128)S(1)}) custom-call(bf16[1,1,384,16384]{3,2,1,0:T(8,128)(2,1)S(1)} %get-tuple-element.10.saved), custom_call_target="tpu_custom_call" | custom-call | tf_op jit(solution)/shard_map/pallas_call | solution.py:251
  264.1 9.2 %shard_map.30.got = bf16[384,1280]{1,0:T(8,128)(2,1)S(1)} custom-call(bf16[384,1280]{1,0:T(8,128)(2,1)S(1)} %get-tuple-element.9.kept, f32[8,128]{1,0:T(8,128)S(1)} %get-tuple-element.11.token), custom_call_target="tpu_custom_call" | custom-call | tf_op jit(solution)/shard_map/pallas_call | solution.py:288
  273.3 0.8 shard_map.31

commit v3 on v2

--- a/solution.py
+++ b/solution.py
@@ -40,7 +40,7 @@
 
 def kernel(n_ep, n_tp, n_dp, chunk, most, weight, span_hbm, out, kept, stage, turned, send, relay, span,
            early, middle, spread, load_sem, span_sem, ep_send, ep_recv, tp_send, tp_recv, late_send, late_recv,
-           early_send, early_recv, fan_send, fan_recv, *arrived):
+           early_send, early_recv, fan_send, fan_recv, settled, ready, *arrived):
     my_ep = lax.axis_index("ep")
     my_tp = lax.axis_index("tp")
     my_dp = lax.axis_index("dp")
@@ -107,35 +107,34 @@
 
     load(0).start()
     barrier = pltpu.get_barrier_semaphore()
-    for d in range(1, n_tp):
-        pl.semaphore_signal(barrier, inc=1, device_id={"tp": lax.rem(my_tp + d, n_tp)}, device_id_type=MESH)
-    for d in range(n_ep - 1, 0, -1):
-        pl.semaphore_signal(barrier, inc=1, device_id={"ep": lax.rem(my_ep + d, n_ep)}, device_id_type=MESH)
+
+    def tell(sem, axis, index):
+        pl.semaphore_signal(sem, inc=1, device_id={axis: index}, device_id_type=MESH)
+
+    ep_peers = [lax.rem(my_ep + d, n_ep) for d in range(n_ep - 1, 0, -1)]
+    tp_peers = [lax.rem(my_tp + d, n_tp) for d in range(1, n_tp)]
+
+    @pl.when(mid)
+    def _():
+        tell(barrier, "tp", n_tp - 1 - my_tp)
+
+    @pl.when(others)
+    def _():
+        for peer in tp_peers:
+            pl.when(jnp.logical_not(middle_of(peer, n_tp)))(functools.partial(tell, barrier, "tp", peer))
+        for peer in ep_peers:
+            tell(barrier, "ep", peer)
+
     span_copy = pltpu.make_async_copy(span_hbm, span, span_sem)
     span_copy.start()
     span_copy.wait()
 
-    wanted = []
-    for d in range(n_ep):
-        i = lax.rem(my_ep + d, n_ep)
-        total = jnp.int32(0)
-        for j in range(n_tp):
-            g = span[i, my_dp, j]
-            total = total + jnp.where(g // per_expert == my_ep, g % per_expert - my_dp * n_tp, 0)
-        wanted.append(total)
-    slot = []
-    for d in [0] + ways:
+    def block_here(g):
+        return jnp.where(lax.div(g, per_expert) == my_ep, lax.rem(g, per_expert) - my_dp * n_tp, 0)
+
+    def sooner(d):
         j = lax.rem(my_tp + d, n_tp)
-        slot.append(lax.rem(my_ep + n_ep - span[my_ep, my_dp, j] // per_expert, n_ep))
-
-    sooner = []
-    for d in [0] + ways:
-        j = lax.rem(my_tp + d, n_tp)
-        total = jnp.int32(0)
-        for i in range(n_ep):
-            g = span[i, my_dp, j]
-            total = total + jnp.where(g // per_expert == my_ep, g % per_expert - my_dp * n_tp, 0)
-        sooner.append(total)
+        return sum((block_here(span[i, my_dp, j]) for i in range(n_ep)), jnp.int32(0))
 
     def turn(c):
         load(c).wait()
@@ -160,7 +159,8 @@
             target[q:q + LANES, :] = pick(tiles, index).T
 
     def first_half(c):
-        turn(c)
+        if c > 1:
+            turn(c)
         for d in range(n_ep - 1, -1, -1):
             if d == 0:
                 arrived[c - 1][0] = block_of(wanted[d])
@@ -186,16 +186,60 @@
         turn(0)
     else:
         load(0).wait()
-    for later in range(1, min(STAGES, chunks)):
-        load(later).start()
-    for k in range(n_tp - 1):
-        first_block(early.at[k], sooner[k + 1])
-        if k == 0:
-            pl.semaphore_wait(barrier, n_ep + n_tp - 2)
-        early_to_tp(k).start()
-    first_block(middle.at[0], sooner[0])
+    def start_loads():
+        for later in range(1, min(STAGES, chunks)):
+            load(later).start()
+
+    later_places = [k for k in range(n_tp - 1) if k != across]
+
+    @pl.when(mid)
+    def _():
+        first_block(early.at[across], sooner(ways[across]))
+        pl.semaphore_wait(barrier, 1)
+        early_to_tp(across).start()
+        start_loads()
+        for peer in tp_peers:
+            pl.when(jnp.logical_not(middle_of(peer, n_tp)))(functools.partial(tell, barrier, "tp", peer))
+        for k in later_places:
+            first_block(early.at[k], sooner(ways[k]))
+        first_block(middle.at[0], sooner(0))
+
+    @pl.when(others)
+    def _():
+        start_loads()
+        for k in range(n_tp - 1):
+            first_block(early.at[k], sooner(ways[k]))
+        first_block(middle.at[0], sooner(0))
+        pl.semaphore_wait(barrier, n_ep + n_tp - 2)
+        for peer in ep_peers:
+            tell(settled, "ep", peer)
+        for k in range(n_tp - 1):
+            early_to_tp(k).start()
+
     if rows % LANES == 0 and STAGES < chunks:
         load(STAGES).start()
+    turn(1)
+
+    wanted = []
+    for d in range(n_ep):
+        i = lax.rem(my_ep + d, n_ep)
+        wanted.append(sum((block_here(span[i, my_dp, j]) for j in range(n_tp)), jnp.int32(0)))
+    slot = []
+    for d in [0] + ways:
+        j = lax.rem(my_tp + d, n_tp)
+        slot.append(lax.rem(my_ep + n_ep - lax.div(span[my_ep, my_dp, j], per_expert), n_ep))
+
+    @pl.when(others)
+    def _():
+        pl.semaphore_wait(settled, n_ep - 1)
+        for peer in tp_peers:
+            pl.when(middle_of(peer, n_tp))(functools.partial(tell, ready, "tp", peer))
+
+    @pl.when(mid)
+    def _():
+        pl.semaphore_wait(ready, n_tp - 2)
+        for k in later_places:
+            early_to_tp(k).start()
 
     for step in range(1, chunks + AHEAD):
         if step < chunks:
@@ -363,6 +407,8 @@
             pltpu.SemaphoreType.DMA,
             pltpu.SemaphoreType.DMA,
             pltpu.SemaphoreType.DMA,
+            pltpu.SemaphoreType.REGULAR,
+            pltpu.SemaphoreType.REGULAR,
         ] + [pltpu.VMEM((n_ep, rows, chunk), kind) for _ in range(chunks - 1)],
         compiler_params=pltpu.CompilerParams(
             collective_id=0, has_side_effects=True, vmem_limit_bytes=VMEM_BYTES - results),

time: 275 us -> 274 us (level)
  no operation moved by 1% of the time
where the time goes in v3:
time: 274 us
  Pallas kernels  274 us (100%)
    pallas_call x1, Pallas kernels, local(): pl.pallas_call(functools.partial(kernel, n_ep, n_tp, n_dp, chunk, most),...  257 us
    pallas_call x1, Pallas kernels, exchange(): pl.pallas_call(functools.partial(swap, n_tp, chunk), out_shape=pltpu.VMEM...  11.2 us

profile of v3, /device:TPU:12, one launch (start us, length us, event | category | flops | bytes accessed | tf_op | source)
XLA Modules:
  0.0 274.0 jit_solution(8945689970299034192)
XLA Ops:
  0.0 257.3 %shard_map.28 = (bf16[1,1,384,16384]{3,2,1,0:T(8,128)(2,1)S(1)}, bf16[384,1280]{1,0:T(8,128)(2,1)S(1)}) custom-call(bf16[1,4096,1536]{2,1,0:T(8,128)(2,1)} %weight.1, s32[4,2,4]{2,1,0:T(2,128)} %bitcast.1), custom_call_target="tpu_custom_call" | custom-call | tf_op jit(solution)/shard_map/pallas_call | solution.py:384
  257.4 4.7 %shard_map.29 = (bf16[1,1,384,16384]{3,2,1,0:T(8,128)(2,1)}, f32[8,128]{1,0:T(8,128)S(1)}) custom-call(bf16[1,1,384,16384]{3,2,1,0:T(8,128)(2,1)S(1)} %get-tuple-element.10.saved), custom_call_target="tpu_custom_call" | custom-call | tf_op jit(solution)/shard_map/pallas_call | solution.py:295
  262.0 11.2 %shard_map.30.got = bf16[384,1280]{1,0:T(8,128)(2,1)S(1)} custom-call(bf16[384,1280]{1,0:T(8,128)(2,1)S(1)} %get-tuple-element.9.kept, f32[8,128]{1,0:T(8,128)S(1)} %get-tuple-element.11.token), custom_call_target="tpu_custom_call" | custom-call | tf_op jit(solution)/shard_map/pallas_call | solution.py:332
  273.3 0.8 shard_map.31

commit v4 on v3

--- a/solution.py
+++ b/solution.py
@@ -16,7 +16,7 @@
 SPARE = 3 << 20
 VMEM_BYTES = 67043328
 WRITES = 8
-KEEP = (2, 5)
+KEEP = (1, 4)
 
 
 def pick(values, index):
@@ -57,8 +57,8 @@
     ways = []
     for k in range(n_tp - 1):
         m = k - (n_tp - 1 - 2 * edge)
-        half = edge - jnp.maximum(m, 0) // 2
-        inner = jnp.where(jnp.maximum(m, 0) % 2 == 0, half, n_tp - half)
+        step = edge - jnp.maximum(m, 0) // 2
+        inner = jnp.where(jnp.maximum(m, 0) % 2 == 0, step, n_tp - step)
         hop = jnp.where(m < 0, n_tp - 1 - edge - k, inner)
         ways.append(jnp.where(near, hop, n_tp - hop))
     across = n_tp - 3
@@ -66,6 +66,12 @@
     def load(c):
         return pltpu.make_async_copy(
             weight.at[0, pl.ds(c * chunk, chunk)], stage.at[c % STAGES], load_sem.at[c % STAGES])
+
+    half = chunk // 2
+
+    def first_load(h):
+        part = pl.ds(h * half, half)
+        return pltpu.make_async_copy(weight.at[0, part], stage.at[0, part], load_sem.at[h * STAGES])
 
     def remote(src, dst, send_sem, recv_sem, axis, d, n):
         me = my_ep if axis == "ep" else my_tp
@@ -105,7 +111,8 @@
     def all_fan():
         return remote(spread, spread, fan_send, fan_recv, "ep", 1, n_ep)
 
-    load(0).start()
+    first_load(0).start()
+    first_load(1).start()
     barrier = pltpu.get_barrier_semaphore()
 
     def tell(sem, axis, index):
@@ -137,7 +144,11 @@
         return sum((block_here(span[i, my_dp, j]) for i in range(n_ep)), jnp.int32(0))
 
     def turn(c):
-        load(c).wait()
+        if c == 0:
+            first_load(0).wait()
+            first_load(1).wait()
+        else:
+            load(c).wait()
 
         @pl.loop(0, width // LANES)
         def _(b):
@@ -182,10 +193,13 @@
                 to_tp(c, k, tp_send, tp_recv).start()
         out[0, 0, :, columns(my_tp, c)] = pick([arrived[c - 1][s] for s in range(n_ep)], slot[0])
 
+    halves = rows % LANES == 0 and half % LANES == 0
     if rows % LANES:
         turn(0)
     else:
-        load(0).wait()
+        first_load(0).wait()
+        if not halves:
+            first_load(1).wait()
     def start_loads():
         for later in range(1, min(STAGES, chunks)):
             load(later).start()
@@ -194,9 +208,24 @@
 
     @pl.when(mid)
     def _():
-        first_block(early.at[across], sooner(ways[across]))
-        pl.semaphore_wait(barrier, 1)
-        early_to_tp(across).start()
+        if halves:
+            index = sooner(ways[across])
+            for h in range(2):
+                part = pl.ds(h * half, half)
+                if h:
+                    first_load(1).wait()
+                for q in range(0, rows, LANES):
+                    tiles = [stage[0, h * half:(h + 1) * half, b * rows + q:b * rows + q + LANES] for b in range(n_tp)]
+                    early[across, q:q + LANES, h * half:(h + 1) * half] = pick(tiles, index).T
+                if h == 0:
+                    pl.semaphore_wait(barrier, 1)
+                remote(
+                    early.at[across, :, part], middle.at[ways[across], :, part], early_send, early_recv,
+                    "tp", ways[across], n_tp).start()
+        else:
+            first_block(early.at[across], sooner(ways[across]))
+            pl.semaphore_wait(barrier, 1)
+            early_to_tp(across).start()
         start_loads()
         for peer in tp_peers:
             pl.when(jnp.logical_not(middle_of(peer, n_tp)))(functools.partial(tell, barrier, "tp", peer))
@@ -206,6 +235,8 @@
 
     @pl.when(others)
     def _():
+        if halves:
+            first_load(1).wait()
         start_loads()
         for k in range(n_tp - 1):
             first_block(early.at[k], sooner(ways[k]))
@@ -395,7 +426,7 @@
             pltpu.VMEM((n_tp - 1, rows, chunk), kind),
             pltpu.VMEM((n_tp, rows, chunk), kind),
             pltpu.VMEM((n_ep - 1, n_tp, rows, chunk), kind),
-            pltpu.SemaphoreType.DMA((STAGES,)),
+            pltpu.SemaphoreType.DMA((STAGES + 1,)),
             pltpu.SemaphoreType.DMA,
             pltpu.SemaphoreType.DMA,
             pltpu.SemaphoreType.DMA((chunks - 1,)),

time: 274 us -> 274 us (level)
    pallas_call x1, Pallas kernels: 11.2 us -> 6.73 us  [exchange(): pl.pallas_call(functools.partial(swap, n_tp, chunk), out_shape=pltpu.VMEM...]
    pallas_call x1, Pallas kernels: 257 us -> 262 us  [local(): pl.pallas_call(functools.partial(kernel, n_ep, n_tp, n_dp, chunk, most),...]
where the time goes in v4:
time: 274 us
  Pallas kernels  274 us (100%)
    pallas_call x1, Pallas kernels, local(): pl.pallas_call(functools.partial(kernel, n_ep, n_tp, n_dp, chunk, most),...  262 us
    pallas_call x1, Pallas kernels, exchange(): pl.pallas_call(functools.partial(swap, n_tp, chunk), out_shape=pltpu.VMEM...  6.73 us

profile of v4, /device:TPU:12, one launch (start us, length us, event | category | flops | bytes accessed | tf_op | source)
XLA Modules:
  0.0 273.8 jit_solution(4032770100118776621)
XLA Ops:
  0.0 261.7 %shard_map.28 = (bf16[1,1,384,16384]{3,2,1,0:T(8,128)(2,1)S(1)}, bf16[384,1024]{1,0:T(8,128)(2,1)S(1)}) custom-call(bf16[1,4096,1536]{2,1,0:T(8,128)(2,1)} %weight.1, s32[4,2,4]{2,1,0:T(2,128)} %bitcast.1), custom_call_target="tpu_custom_call" | custom-call | tf_op jit(solution)/shard_map/pallas_call | solution.py:415
  261.7 4.7 %shard_map.29 = (bf16[1,1,384,16384]{3,2,1,0:T(8,128)(2,1)}, f32[8,128]{1,0:T(8,128)S(1)}) custom-call(bf16[1,1,384,16384]{3,2,1,0:T(8,128)(2,1)S(1)} %get-tuple-element.10.saved), custom_call_target="tpu_custom_call" | custom-call | tf_op jit(solution)/shard_map/pallas_call | solution.py:326
  266.3 6.7 %shard_map.30.got = bf16[384,1024]{1,0:T(8,128)(2,1)S(1)} custom-call(bf16[384,1024]{1,0:T(8,128)(2,1)S(1)} %get-tuple-element.9.kept, f32[8,128]{1,0:T(8,128)S(1)} %get-tuple-element.11.token), custom_call_target="tpu_custom_call" | custom-call | tf_op jit(solution)/shard_map/pallas_call | solution.py:363
  273.1 0.7 shard_map.31
